TPU v7x, 128 devices: a whole 4x4x4 slice. The times are simulated.
128 devices in a mesh: node: 16 (over z, y), dev: 8 (over x, core).
Axes of the slice: x: 4, y: 4, z: 4, core: 2. Of those that a mesh axis runs over, the one named last changes fastest.
Arguments:
- tokens: bfloat16 [8192, 5120], P(('node', 'dev')), may hold values from -6 to 6
- node_ids: int32 [8192, 3], P(('node', 'dev')), may hold values from 0 to 15, all different within a row; in each aligned block of 64 rows (0 to 63, 64 to 127, ...) at most 13 rows name the same one
- expert_pick: int32 [8192, 6], P(('node', 'dev')), may hold values from 0 to 8, all different within a row
- gate_share: bfloat16 [8192, 6], P(('node', 'dev')), may hold values from 0.099609375 to 1
- gate_proj: bfloat16 [48, 1536, 5120], P('node', 'dev'), may hold values from -0.078125 to 0.078125
- up_proj: bfloat16 [48, 1536, 5120], P('node', 'dev'), may hold values from -0.078125 to 0.078125
- down_proj: bfloat16 [48, 1536, 5120], P('node', 'dev'), may hold values from -0.15625 to 0.15625
Outputs:
- moe_out: bfloat16 [8192, 5120], P(('node', 'dev'))
Inputs may be any that keep to these rules, and one draw needn't show every extreme that they name: `node_ids`: A token names 3 different groups; at most 13 tokens of one device name one group, and some device reaches 13 in every draw. `expert_pick`: A token names 6 different picks; pick p selects local expert p % 3 of the token's group choice p // 3.
All inputs are finite; a program needn't handle non-finite values.
Results may differ from a plain program's by a relative error of at most 0.0085.
Values may be sent and summed in bfloat16 or wider, within the bound.
A program may use at most 256 MiB of HBM per device.

v0:
```python
import functools
import math

import jax
import jax.numpy as jnp
from jax import lax
from jax.experimental import pallas as pl
from jax.experimental.pallas import tpu as pltpu
from jax.sharding import PartitionSpec as P

LANES = 128
SLOTS = 16
CAP = 13
BLOCK = 64
F32 = jnp.float32
BF16 = jnp.bfloat16
MESH = pl.DeviceIdType.MESH
CUTS = (0, 48, 96, 160, 208)
HOPS = (
    (0, 0), (0, 1), (1, 0), (0, 3), (3, 0), (1, 1), (1, 2), (2, 1),
    (2, 2), (2, 3), (3, 2), (0, 2), (2, 0), (1, 3), (3, 1), (3, 3),
)


def kernel(
    send_ref, gate_ref, up_ref, down_ref, back_ref,
    wgu, wd, xbuf, exr, pr, ra, rb, fl, fr, hbuf,
    wsem, exs, exv, ags, agv, rss, rsv, rts, rtv,
):
    local, hidden, width = gate_ref.shape
    nodes = len(HOPS)
    side = math.isqrt(nodes)
    half = width // 2
    tiles = wgu.shape[0]
    node = lax.axis_index("node")
    dev = lax.axis_index("dev")
    z, y = node // side, node % side
    ring = 4
    cx, core = dev // 2, dev % 2
    right = {"dev": (cx + 1) % ring * 2 + core}
    left = {"dev": (cx + ring - 1) % ring * 2 + core}
    partner = {"dev": cx * 2 + (1 - core)}

    def there(p):
        dz, dy = HOPS[p]
        return {"node": (z + dz) % side * side + (y + dy) % side}

    def back_there(p):
        dz, dy = HOPS[p]
        return {"node": (z + side - dz) % side * side + (y + side - dy) % side}

    def remote(src, dst, ssem, rsem, device):
        return pltpu.make_async_remote_copy(
            src_ref=src, dst_ref=dst, send_sem=ssem, recv_sem=rsem,
            device_id=device, device_id_type=MESH,
        )

    weights = []
    for e in range(local):
        for b in range(hidden // BLOCK):
            blk = e * (hidden // BLOCK) + b
            i, at = blk // 2, blk % 2 * BLOCK
            rows = pl.ds(b * BLOCK, BLOCK)
            weights.append((gate_ref.at[e, rows], wgu.at[i, pl.ds(at, BLOCK)]))
            weights.append((up_ref.at[e, rows], wgu.at[i, pl.ds(LANES + at, BLOCK)]))
        weights.append((down_ref.at[e], wd.at[pl.ds(e * hidden, hidden)]))
    weights = [
        pltpu.make_async_copy(s, d, wsem.at[i]) for i, (s, d) in enumerate(weights)
    ]

    barrier = pltpu.get_barrier_semaphore()
    for p in range(1, nodes):
        pl.semaphore_signal(barrier, inc=1, device_id=there(p), device_id_type=MESH)
    for device in (right, left, partner):
        pl.semaphore_signal(barrier, inc=1, device_id=device, device_id_type=MESH)
    own_in = pltpu.make_async_copy(send_ref.at[0], exr.at[pl.ds(0, SLOTS)], exs.at[0])
    own_in.start()
    for w in weights:
        w.start()
    used = local * hidden
    if used < tiles * LANES:
        rest = tiles * LANES - used
        wgu[tiles - 1, LANES - rest : LANES] = jnp.zeros((rest, width), BF16)
        wgu[tiles - 1, 2 * LANES - rest :] = jnp.zeros((rest, width), BF16)
        wd[used:] = jnp.zeros((rest, width), BF16)
    pl.semaphore_wait(barrier, nodes + 2)

    exchange = {}
    for p in range(1, nodes):
        exchange[p] = remote(
            send_ref.at[p], exr.at[pl.ds(p * SLOTS, SLOTS)], exs.at[p], exv.at[p], there(p)
        )
        exchange[p].start()

    chunks = list(zip(CUTS[:-1], CUTS[1:]))
    ag = [{} for _ in chunks]
    rs = [{} for _ in chunks]
    state = {"arrived": 0, "returned": 0}
    ret = {}

    def onehot(rows, cols, hit):
        i = lax.broadcasted_iota(jnp.int32, (rows, cols), 0)
        j = lax.broadcasted_iota(jnp.int32, (rows, cols), 1)
        return hit(i, j).astype(F32).astype(BF16)

    def own(c):
        a, b = chunks[c]
        n0, n1 = a // CAP, (b - 1) // CAP + 1
        while state["arrived"] < n1:
            p = state["arrived"]
            if p == 0:
                own_in.wait()
            else:
                exchange[p].wait_recv()
            state["arrived"] += 1
        def hit(i, j):
            match = None
            for p in range(n0, n1):
                k = j - (p - n0) * SLOTS
                m = (k >= 0) & (k < CAP) & (i + a == k + p * CAP)
                match = m if match is None else match | m
            return match

        pick = onehot(b - a, (n1 - n0) * SLOTS, hit)
        dense = jnp.dot(
            pick, exr[n0 * SLOTS : n1 * SLOTS, :], preferred_element_type=F32
        )
        xbuf[0, a:b, :] = dense.astype(BF16)
        rows = pl.ds(a, b - a)
        mine = xbuf.at[0, rows]
        ag[c][0] = remote(mine, xbuf.at[3, rows], ags.at[c, 0], agv.at[c, 0], right)
        ag[c][1] = remote(mine, xbuf.at[1, rows], ags.at[c, 1], agv.at[c, 1], left)
        ag[c][2] = remote(mine, xbuf.at[4, rows], ags.at[c, 2], agv.at[c, 2], partner)
        for q in range(3):
            ag[c][q].start()

    def relay(c):
        a, b = chunks[c]
        rows = pl.ds(a, b - a)
        low, high = pl.ds(0, half), pl.ds(half, xbuf.shape[2] - half)
        ag[c][3] = remote(
            xbuf.at[3, rows, low], xbuf.at[2, rows, low], ags.at[c, 3], agv.at[c, 3], right
        )
        ag[c][4] = remote(
            xbuf.at[1, rows, high], xbuf.at[2, rows, high], ags.at[c, 4], agv.at[c, 4], left
        )
        for q, s in ((5, 3), (6, 1), (7, 2)):
            ag[c][q] = remote(
                xbuf.at[s, rows], xbuf.at[4 + s, rows], ags.at[c, q], agv.at[c, q], partner
            )
        ag[c][0].wait_recv()
        ag[c][3].start()
        ag[c][5].start()
        ag[c][1].wait_recv()
        ag[c][4].start()
        ag[c][6].start()

    def far(c):
        ag[c][3].wait_recv()
        ag[c][4].wait_recv()
        ag[c][7].start()
        for q in (2, 5, 6, 7):
            ag[c][q].wait_recv()

    def compute(c):
        a, b = chunks[c]
        span = b - a
        count = 8 * span

        def hidden_tile(i, _):
            x = xbuf[:, a:b, :width].reshape(count, width)
            acc = lax.dot_general(
                x, wgu[i], (((1,), (1,)), ((), ())), preferred_element_type=F32
            )
            g, u = acc[:, :LANES], acc[:, LANES:]
            shares = xbuf[:, a:b, width:].reshape(count, LANES)

            def hit(e, j):
                at = j + i * LANES - e * hidden
                return (at >= 0) & (at < hidden) & (e < local)

            scale = jnp.dot(
                shares, onehot(LANES, LANES, hit), preferred_element_type=F32
            )
            h = g / (1.0 + jnp.exp(-g)) * u * scale
            hbuf[:count, pl.ds(pl.multiple_of(i * LANES, LANES), LANES)] = h.astype(BF16)
            return _

        lax.fori_loop(0, tiles, hidden_tile, 0)
        for q in range(8):
            ag[c][q].wait_send()

        tile = 512

        def down_tile(n, _):
            cols = pl.ds(pl.multiple_of(n * tile, tile), tile)
            out = jnp.dot(hbuf[:count, :], wd[:, cols], preferred_element_type=F32)
            xbuf[:, a:b, cols] = out.astype(BF16).reshape(8, span, tile)
            return _

        lax.fori_loop(0, width // tile, down_tile, 0)
        rows, cols = pl.ds(a, span), pl.ds(0, width)
        rs[c][0] = remote(
            xbuf.at[pl.ds(4, 4), rows, cols], pr.at[:, rows], rss.at[c, 0], rsv.at[c, 0], partner
        )
        rs[c][0].start()

    def add(dst, dst_at, srcs, a, b, low, high):
        tile = 512

        def step(n, _):
            cols = pl.ds(pl.multiple_of(low + n * tile, tile), tile)
            total = dst[dst_at, a:b, cols].astype(F32)
            for src in srcs:
                total = total + src(n * tile, tile).astype(F32)
            dst[dst_at, a:b, cols] = total.astype(BF16)
            return _

        lax.fori_loop(0, (high - low) // tile, step, 0)

    def cut(ref, lead, a, b, base):
        def get(at, size):
            cols = pl.ds(pl.multiple_of(base + at, size), size)
            return ref[a:b, cols] if lead is None else ref[lead, a:b, cols]

        return get

    def partner_sum(c):
        a, b = chunks[c]
        rows = pl.ds(a, b - a)
        low, high = pl.ds(0, half), pl.ds(half, half)
        rs[c][0].wait_recv()
        rs[c][1] = remote(xbuf.at[2, rows, low], ra.at[rows], rss.at[c, 1], rsv.at[c, 1], right)
        rs[c][2] = remote(xbuf.at[2, rows, high], rb.at[rows], rss.at[c, 2], rsv.at[c, 2], left)
        rs[c][3] = remote(
            xbuf.at[1, rows, high], fl.at[rows, high], rss.at[c, 3], rsv.at[c, 3], right
        )
        rs[c][4] = remote(
            xbuf.at[3, rows, low], fr.at[rows, low], rss.at[c, 4], rsv.at[c, 4], left
        )
        rs[c][5] = remote(
            xbuf.at[1, rows, low], fl.at[rows, low], rss.at[c, 5], rsv.at[c, 5], right
        )
        rs[c][6] = remote(
            xbuf.at[3, rows, high], fr.at[rows, high], rss.at[c, 6], rsv.at[c, 6], left
        )
        add(xbuf, 2, [cut(pr, 2, a, b, 0)], a, b, 0, width)
        rs[c][1].start()
        rs[c][2].start()
        add(xbuf, 1, [cut(pr, 1, a, b, 0)], a, b, 0, width)
        rs[c][3].start()
        add(xbuf, 3, [cut(pr, 3, a, b, 0)], a, b, 0, width)
        rs[c][4].start()
        add(xbuf, 0, [cut(pr, 0, a, b, 0)], a, b, 0, width)

    def ring_sum(c):
        a, b = chunks[c]
        rs[c][1].wait_recv()
        add(xbuf, 1, [cut(ra, None, a, b, 0)], a, b, 0, half)
        rs[c][5].start()
        rs[c][2].wait_recv()
        add(xbuf, 3, [cut(rb, None, a, b, 0)], a, b, half, width)
        rs[c][6].start()

    def finish(c):
        a, b = chunks[c]
        for q in (3, 4, 5, 6):
            rs[c][q].wait_recv()
        add(xbuf, 0, [cut(fl, None, a, b, 0), cut(fr, None, a, b, 0)], a, b, 0, width)
        p0 = state["returned"]
        p1 = b // CAP
        state["returned"] = p1
        w0 = p0 * CAP // 16 * 16

        def hit(i, j):
            match = None
            for p in range(p0, p1):
                s = i - (p - p0) * SLOTS
                m = (s >= 0) & (s < CAP) & (j + w0 == s + p * CAP)
                match = m if match is None else match | m
            return match

        spread = onehot((p1 - p0) * SLOTS, b - w0, hit)
        tile = 1280

        def step(n, _):
            cols = pl.ds(pl.multiple_of(n * tile, tile), tile)
            out = jnp.dot(spread, xbuf[0, w0:b, cols], preferred_element_type=F32)
            exr[p0 * SLOTS : p1 * SLOTS, cols] = out.astype(BF16)
            return _

        lax.fori_loop(0, width // tile, step, 0)
        for p in range(p0, p1):
            src = exr.at[pl.ds(p * SLOTS, SLOTS), pl.ds(0, width)]
            if p == 0:
                ret[p] = pltpu.make_async_copy(src, back_ref.at[0], rts.at[0])
            else:
                ret[p] = remote(src, back_ref.at[p], rts.at[p], rtv.at[p], back_there(p))
            ret[p].start()

    last = len(chunks) - 1
    own(0)
    own(1)
    relay(0)
    own(2)
    for w in weights:
        w.wait()
    for c in range(len(chunks)):
        far(c)
        compute(c)
        if c + 1 <= last:
            relay(c + 1)
        if c + 3 <= last:
            own(c + 3)
        partner_sum(c)
        if c >= 1:
            ring_sum(c - 1)
        if c >= 2:
            finish(c - 2)
    ring_sum(last)
    finish(last - 1)
    finish(last)
    for p in range(1, nodes):
        exchange[p].wait_send()
    for c in range(len(chunks)):
        for q in range(7):
            rs[c][q].wait_send()
    ret[0].wait()
    for p in range(1, nodes):
        ret[p].wait_send()
        ret[p].wait_recv()


def routed(send, gate_proj, up_proj, down_proj):
    nodes, slots, ext = send.shape
    local, hidden, width = gate_proj.shape
    rows = nodes * CAP
    chunks = len(CUTS) - 1
    most = max(b - a for a, b in zip(CUTS[:-1], CUTS[1:]))
    tiles = -(-local * hidden // LANES)
    dma = pltpu.SemaphoreType.DMA
    return pl.pallas_call(
        kernel,
        out_shape=jax.ShapeDtypeStruct((nodes, slots, width), BF16),
        in_specs=[pl.BlockSpec(memory_space=pl.ANY)] * 4,
        out_specs=pl.BlockSpec(memory_space=pl.ANY),
        scratch_shapes=[
            pltpu.VMEM((tiles, 2 * LANES, width), BF16),
            pltpu.VMEM((tiles * LANES, width), BF16),
            pltpu.VMEM((8, rows, ext), BF16),
            pltpu.VMEM((nodes * slots, ext), BF16),
            pltpu.VMEM((4, rows, width), BF16),
            pltpu.VMEM((rows, width // 2), BF16),
            pltpu.VMEM((rows, width // 2), BF16),
            pltpu.VMEM((rows, width), BF16),
            pltpu.VMEM((rows, width), BF16),
            pltpu.VMEM((8 * most, tiles * LANES), BF16),
            dma((local * (2 * (hidden // BLOCK) + 1),)),
            dma((nodes,)),
            dma((nodes,)),
            dma((chunks, 8)),
            dma((chunks, 8)),
            dma((chunks, 7)),
            dma((chunks, 7)),
            dma((nodes,)),
            dma((nodes,)),
        ],
        compiler_params=pltpu.CompilerParams(
            collective_id=0, has_side_effects=True, vmem_limit_bytes=67_043_328
        ),
        name="routed_experts",
    )(send, gate_proj, up_proj, down_proj)


def shards(tokens, node_ids, expert_pick, gate_share, gate_proj, up_proj, down_proj):
    tok_count, width = tokens.shape
    nodes = lax.axis_size("node")
    side = math.isqrt(nodes)
    me = lax.axis_index("node")
    choices = node_ids.shape[1]
    local = gate_proj.shape[0]

    hop = jnp.array(HOPS, jnp.int32)
    order = (me // side + hop[:, 0]) % side * side + (me % side + hop[:, 1]) % side
    picked = (
        expert_pick[:, :, None] == jnp.arange(choices * local, dtype=jnp.int32)[None, None, :]
    )
    shares = jnp.sum(jnp.where(picked, gate_share[:, :, None].astype(F32), 0.0), axis=1)
    shares = shares.reshape(tok_count, choices, local)
    chosen = node_ids[:, :, None] == order[None, None, :]
    gates = jnp.sum(
        jnp.where(chosen[:, :, :, None], shares[:, :, None, :], 0.0), axis=1
    )
    mask = jnp.any(chosen, axis=1)
    at = jnp.arange(tok_count, dtype=jnp.int32)
    earlier = (at[None, :] < at[:, None]).astype(BF16)
    before = jnp.dot(earlier, mask.astype(BF16), preferred_element_type=F32).astype(jnp.int32)
    slot_of = jnp.where(mask, before, -1)
    select = (
        slot_of.T[:, None, :] == jnp.arange(SLOTS, dtype=jnp.int32)[None, :, None]
    ).astype(BF16)
    flat = select.reshape(nodes * SLOTS, tok_count)
    feats = jnp.dot(flat, tokens, preferred_element_type=F32).astype(BF16)
    gate_rows = jnp.einsum(
        "pst,tpe->pse", select, gates.astype(BF16), preferred_element_type=F32
    ).astype(BF16)
    gate_rows = jnp.pad(gate_rows, ((0, 0), (0, 0), (0, LANES - local)))
    send = jnp.concatenate([feats.reshape(nodes, SLOTS, width), gate_rows], axis=2)

    back = routed(send, gate_proj, up_proj, down_proj)
    total = lax.dot_general(
        flat, back.reshape(nodes * SLOTS, width), (((0,), (0,)), ((), ())),
        preferred_element_type=F32,
    )
    return total.astype(BF16)


def solution(mesh):
    return jax.shard_map(
        shards,
        mesh=mesh,
        in_specs=(
            P(("node", "dev"), None),
            P(("node", "dev"), None),
            P(("node", "dev"), None),
            P(("node", "dev"), None),
            P("node", "dev", None),
            P("node", "dev", None),
            P("node", "dev", None),
        ),
        out_specs=P(("node", "dev"), None),
        check_vma=False,
    )
```

profile of v0, /device:TPU:34, one launch (start us, length us, event | category | flops | bytes accessed | tf_op | source)
XLA Modules:
  0.0 209.4 jit_solution(12590737663921937692)
XLA Ops:
  0.0 0.7 fusion.8
  0.7 0.7 convert_element_type.27
  1.4 0.7 select_reduce_fusion.1
  2.1 0.8 broadcast_compare_fusion
  2.9 0.1 fusion.3
  3.0 0.0 copy-start
  3.0 0.2 fusion.4
  3.2 0.1 eq.67
  3.3 0.3 copy-done
  3.6 0.1 bitcast_compare_fusion
  3.7 0.2 copy.20
  3.9 1.9 convolution_convert_fusion
  5.8 1.7 fusion.2.send_ref
  7.5 198.6 %routed_experts.1 = bf16[16,16,5120]{2,1,0:T(8,128)(2,1)} custom-call(bf16[16,16,5248]{2,1,0:T(8,128)(2,1)} %fusion.2.send_ref, bf16[3,192,5120]{2,1,0:T(8,128)(2,1)} %gate_ref.1, bf16[3,192,5120]{2,1,0:T(8,128)(2,1)} %up_ref.1, bf16[3,192,5120]{2,1,0:T(8,128)(2,1)} %down_ref.1), custom_call_target="tpu_custom_call" | custom-call | tf_op jit(solution)/shard_map/routed_experts/pallas_call | solution.py:342
  206.2 3.2 %fusion = bf16[64,5120]{1,0:T(8,128)(2,1)} fusion(bf16[16,16,5120]{2,1,0:T(8,128)(2,1)} %routed_experts.1, s32[16,64]{1,0:T(8,128)} %copy-done), kind=kOutput, calls=%fused_computation.2 | convolution fusion | flops 168116224 | bytes 3280896 | tf_op jit(solution)/shard_map/dot_general | solution.py:411
  (4 shorter events, 0.0 us)
Async XLA Ops:
  3.0 0.6 copy-start
where the time goes:
time: 210 us; the launch traced here: 209 us
  Pallas kernels  199 us (95%)
  matrix products  5.41 us (3%)
  other arithmetic  4.68 us (2%)
    pallas_call x1, Pallas kernels, routed(): pl.pallas_call(kernel, out_shape=jax.ShapeDtypeStruct((nodes, slots, widt...  199 us

commit v1 on v0

v1 whole, which is shorter than its diff:
```python
import math

import jax
import jax.numpy as jnp
from jax import lax
from jax.experimental import pallas as pl
from jax.experimental.pallas import tpu as pltpu
from jax.sharding import PartitionSpec as P

LANES = 128
SLOTS = 16
CAP = 13
BLOCK = 64
WB = 512
F32 = jnp.float32
BF16 = jnp.bfloat16
MESH = pl.DeviceIdType.MESH
CUTS = (0, 48, 112, 176, 208)
HOPS = (
    (0, 0), (0, 1), (1, 0), (0, 3), (1, 1), (3, 3), (0, 2), (2, 0),
    (1, 2), (2, 3), (2, 1), (3, 2), (2, 2), (3, 1), (1, 3), (3, 0),
)


def kernel(
    ids_ref, pick_ref, share_ref, tok_ref, gate_ref, up_ref, down_ref, out_ref,
    tbuf, sbuf, tb, pb, selb, xs, er, back, wgu, wd, xbuf, exr, pr, ra, rb, fl, fr, hbuf,
    tsem, tss, trs, bxs, bxr, wsem, exs, exv, ags, agv, rss, rsv, rts, rtv,
):
    local, hidden, width = gate_ref.shape
    nodes = len(HOPS)
    side = math.isqrt(nodes)
    half = width // 2
    da = width - 2 * WB
    ext = da + LANES
    tiles = wgu.shape[0]
    node = lax.axis_index("node")
    dev = lax.axis_index("dev")
    z, y = node // side, node % side
    ring = 4
    cx, core = dev // 2, dev % 2
    right = {"dev": (cx + 1) % ring * 2 + core}
    left = {"dev": (cx + ring - 1) % ring * 2 + core}
    partner = {"dev": cx * 2 + (1 - core)}

    def there(p):
        dz, dy = HOPS[p]
        return {"node": (z + dz) % side * side + (y + dy) % side}

    def back_there(p):
        dz, dy = HOPS[p]
        return {"node": (z + side - dz) % side * side + (y + side - dy) % side}

    def remote(src, dst, ssem, rsem, device):
        return pltpu.make_async_remote_copy(
            src_ref=src, dst_ref=dst, send_sem=ssem, recv_sem=rsem,
            device_id=device, device_id_type=MESH,
        )

    mine_at = pl.multiple_of(da + core * WB, LANES)
    other_at = pl.multiple_of(da + (1 - core) * WB, LANES)
    pieces = (
        (pl.ds(0, da), pl.ds(0, da)),
        (pl.ds(mine_at, WB), pl.ds(da, WB)),
        (pl.ds(other_at, WB), pl.ds(da + WB, WB)),
    )

    weights = []
    for e in range(local):
        for b in range(hidden // BLOCK):
            blk = e * (hidden // BLOCK) + b
            i, at = blk // 2, blk % 2 * BLOCK
            rows = pl.ds(b * BLOCK, BLOCK)
            for src, dst in pieces:
                weights.append(
                    (gate_ref.at[e, rows, src], wgu.at[i, pl.ds(at, BLOCK), dst])
                )
                weights.append(
                    (up_ref.at[e, rows, src], wgu.at[i, pl.ds(LANES + at, BLOCK), dst])
                )
        weights.append((down_ref.at[e], wd.at[pl.ds(e * hidden, hidden)]))
    weights = [
        pltpu.make_async_copy(s, d, wsem.at[i]) for i, (s, d) in enumerate(weights)
    ]

    barrier = pltpu.get_barrier_semaphore()
    for p in range(1, nodes):
        pl.semaphore_signal(barrier, inc=1, device_id=there(p), device_id_type=MESH)
    for device in (right, left, partner):
        pl.semaphore_signal(barrier, inc=1, device_id=device, device_id_type=MESH)
    token_copies = [
        pltpu.make_async_copy(tok_ref.at[:, src], tbuf.at[:, dst], tsem.at[i])
        for i, (src, dst) in enumerate(pieces)
    ]
    for copy in token_copies:
        copy.start()
    for w in weights:
        w.start()
    used = local * hidden
    if used < tiles * LANES:
        rest = tiles * LANES - used
        wgu[tiles - 1, LANES - rest : LANES] = jnp.zeros((rest, width), BF16)
        wgu[tiles - 1, 2 * LANES - rest :] = jnp.zeros((rest, width), BF16)
        wd[used:] = jnp.zeros((rest, width), BF16)
    def onehot(rows, cols, hit):
        i = lax.broadcasted_iota(jnp.int32, (rows, cols), 0)
        j = lax.broadcasted_iota(jnp.int32, (rows, cols), 1)
        return hit(i, j).astype(F32).astype(BF16)

    count_tok, choices = ids_ref.shape
    wide = (count_tok, nodes * SLOTS)
    lane = lax.broadcasted_iota(jnp.int32, wide, 1)
    group, slot = lane // SLOTS, lane % SLOTS
    order = jnp.zeros(wide, jnp.int32)
    for p in range(nodes):
        order = jnp.where(group == p, there(p)["node"], order)
    hits = [ids_ref[:, m : m + 1] == order for m in range(choices)]
    mask = hits[0]
    for m in range(1, choices):
        mask = mask | hits[m]
    earlier = onehot(count_tok, count_tok, lambda i, j: j < i)
    rank = jnp.dot(earlier, mask.astype(F32).astype(BF16), preferred_element_type=F32)
    select = jnp.where(mask & (rank == slot.astype(F32)), 1.0, 0.0)
    rows_of = select.T.astype(BF16)
    gate_rows = jnp.zeros((nodes * SLOTS, LANES), F32)
    for e in range(local):
        gates = jnp.zeros(wide, F32)
        for m in range(choices):
            share = jnp.zeros((count_tok, 1), F32)
            for k in range(pick_ref.shape[1]):
                share = share + jnp.where(
                    pick_ref[:, k : k + 1] == m * local + e,
                    share_ref[:, k : k + 1].astype(F32),
                    0.0,
                )
            gates = gates + jnp.where(hits[m], share, 0.0)
        gate_rows = gate_rows + jnp.dot(
            (select * gates).T.astype(BF16),
            onehot(count_tok, LANES, lambda i, j: j == e),
            preferred_element_type=F32,
        )
    sbuf[:, da:] = gate_rows.astype(BF16)
    spread_rows = select.astype(BF16)
    slots_of = jnp.dot(
        jnp.where(mask, rank, -1.0).astype(BF16),
        onehot(nodes * SLOTS, LANES, lambda i, j: i == j * SLOTS),
        preferred_element_type=F32,
    )
    slots_of = jnp.where(
        lax.broadcasted_iota(jnp.int32, slots_of.shape, 1) < nodes, slots_of, -1.0
    ).astype(BF16)
    for copy in token_copies:
        copy.wait()
    tb[0, :count_tok, :WB] = tbuf[:, da : da + WB]
    tb[0, :count_tok, WB:] = slots_of
    pb[:, :WB] = tbuf[:, da + WB :]
    pb[:, WB:] = slots_of

    def pack(n, _):
        cols = pl.ds(pl.multiple_of(n * 1024, 1024), 1024)
        sbuf[:, cols] = jnp.dot(
            rows_of, tbuf[:, cols], preferred_element_type=F32
        ).astype(BF16)
        return _

    lax.fori_loop(0, da // 1024, pack, 0)
    exr[:SLOTS, :ext] = sbuf[:SLOTS, :]
    pl.semaphore_wait(barrier, nodes + 2)

    first, second = pl.ds(0, count_tok), pl.ds(count_tok, count_tok)
    row = [
        remote(pb, tb.at[0, second], tss.at[0], trs.at[0], partner),
        remote(tb.at[0, first], tb.at[3, first], tss.at[1], trs.at[1], right),
        remote(tb.at[0, second], tb.at[3, second], tss.at[2], trs.at[2], right),
        remote(tb.at[0, second], tb.at[1, second], tss.at[3], trs.at[3], left),
        remote(tb.at[0, first], tb.at[1, first], tss.at[4], trs.at[4], left),
        remote(tb.at[3, first], tb.at[2, first], tss.at[5], trs.at[5], right),
        remote(tb.at[1, second], tb.at[2, second], tss.at[6], trs.at[6], left),
    ]
    for q in (0, 1, 4):
        row[q].start()
    exchange = {}

    def exchange_rows(c):
        p0, p1 = starts[c], starts[c + 1]
        for p in range(max(p0, 1), p1):
            block = pl.ds(p * SLOTS, SLOTS)
            exchange[p] = remote(
                sbuf.at[block], exr.at[block, pl.ds(0, ext)], exs.at[p], exv.at[p], there(p)
            )
            exchange[p].start()

    chunks = list(zip(CUTS[:-1], CUTS[1:]))
    starts = [0] + [(b - 1) // CAP + 1 for _, b in chunks]
    ag = [{} for _ in chunks]
    rs = [{} for _ in chunks]
    state = {"arrived": 0, "returned": 0}
    ret = {}

    low, high = pl.ds(0, half), pl.ds(half, half)
    ag_low, ag_high, ag_all = pl.ds(0, da // 2), pl.ds(da // 2, ext - da // 2), pl.ds(0, ext)
    bsend = {}

    def selectors(dx):
        for dc in range(2):
            vals = tb[dx, dc * count_tok : (dc + 1) * count_tok, WB:]
            wanted = jnp.dot(
                vals,
                onehot(LANES, nodes * SLOTS, lambda i, j: i == j // SLOTS),
                preferred_element_type=F32,
            )
            hit = jnp.where(wanted == slot.astype(F32), 1.0, 0.0)
            selb[dx * 2 + dc] = hit.T.astype(BF16)

    def build(c):
        p0, p1 = starts[c], starts[c + 1]
        if c >= 2:
            for p in range(max(starts[c - 2], 1), starts[c - 1]):
                bsend[p].wait_send()
        for k in range(8):
            tok = tb[k // 2, k % 2 * count_tok : (k % 2 + 1) * count_tok, :WB]
            rows = jnp.dot(
                selb[k, p0 * SLOTS : p1 * SLOTS, :], tok, preferred_element_type=F32
            ).astype(BF16)
            rows = rows.reshape(p1 - p0, SLOTS, WB)
            if p0 == 0:
                er[0, k] = rows[0]
            xs[c % 2, : p1 - p0, k] = rows
        for p in range(max(p0, 1), p1):
            bsend[p] = remote(
                xs.at[c % 2, p - p0], er.at[p], bxs.at[p], bxr.at[p], there(p)
            )
            bsend[p].start()

    def picker(c):
        a, b = chunks[c]
        n0, n1 = a // CAP, (b - 1) // CAP + 1

        def hit(i, j):
            match = None
            for p in range(n0, n1):
                k = j - (p - n0) * SLOTS
                m = (k >= 0) & (k < CAP) & (i + a == k + p * CAP)
                match = m if match is None else match | m
            return match

        return onehot(b - a, (n1 - n0) * SLOTS, hit), n0, n1

    def take(c):
        a, b = chunks[c]
        for p in range(max(starts[c], 1), starts[c + 1]):
            bsend[p].wait_recv()
        pick, n0, n1 = picker(c)
        for k in range(8):
            src = er[n0:n1, k].reshape((n1 - n0) * SLOTS, WB)
            xbuf[k % 2 * 4 + k // 2, a:b, ext : ext + WB] = jnp.dot(
                pick, src, preferred_element_type=F32
            ).astype(BF16)
        rows = pl.ds(a, b - a)
        for q, s in ((10, 0), (11, 4)):
            ag[c][q] = remote(
                xbuf.at[pl.ds(s, 4), rows, pl.ds(ext, WB)],
                xbuf.at[pl.ds(4 - s, 4), rows, pl.ds(ext + WB, WB)],
                ags.at[c, q], agv.at[c, q], partner,
            )
            ag[c][q].start()

    def own(c):
        a, b = chunks[c]
        for p in range(max(starts[c], 1), starts[c + 1]):
            exchange[p].wait_recv()
        pick, n0, n1 = picker(c)
        dense = jnp.dot(
            pick, exr[n0 * SLOTS : n1 * SLOTS, :ext], preferred_element_type=F32
        )
        xbuf[0, a:b, :ext] = dense.astype(BF16)
        rows = pl.ds(a, b - a)
        for q, s, cols, device in (
            (0, 3, ag_low, right), (2, 1, ag_high, left),
            (1, 3, ag_high, right), (3, 1, ag_low, left),
        ):
            ag[c][q] = remote(
                xbuf.at[0, rows, cols], xbuf.at[s, rows, cols], ags.at[c, q], agv.at[c, q], device
            )
            ag[c][q].start()
        ag[c][4] = remote(
            xbuf.at[0, rows, ag_all], xbuf.at[4, rows, ag_all], ags.at[c, 4], agv.at[c, 4], partner
        )
        ag[c][4].start()

    def relay(c):
        a, b = chunks[c]
        rows = pl.ds(a, b - a)
        ag[c][5] = remote(
            xbuf.at[3, rows, ag_low], xbuf.at[2, rows, ag_low], ags.at[c, 5], agv.at[c, 5], right
        )
        ag[c][6] = remote(
            xbuf.at[1, rows, ag_high], xbuf.at[2, rows, ag_high], ags.at[c, 6], agv.at[c, 6], left
        )
        ag[c][0].wait_recv()
        ag[c][5].start()
        ag[c][2].wait_recv()
        ag[c][6].start()

    def forward(c):
        a, b = chunks[c]
        rows = pl.ds(a, b - a)
        for q, s, ready in ((7, 3, 1), (8, 1, 3)):
            ag[c][ready].wait_recv()
            ag[c][q] = remote(
                xbuf.at[s, rows, ag_all], xbuf.at[4 + s, rows, ag_all],
                ags.at[c, q], agv.at[c, q], partner,
            )
            ag[c][q].start()

    def far(c):
        a, b = chunks[c]
        rows = pl.ds(a, b - a)
        ag[c][5].wait_recv()
        ag[c][6].wait_recv()
        ag[c][9] = remote(
            xbuf.at[2, rows, ag_all], xbuf.at[6, rows, ag_all], ags.at[c, 9], agv.at[c, 9], partner
        )
        ag[c][9].start()
        for q in (4, 7, 8, 9, 10, 11):
            ag[c][q].wait_recv()

    def gated(c, first, count_tiles):
        a, b = chunks[c]
        span = b - a
        count = 8 * span

        def hidden_tile(i, _):
            contract = (((1,), (1,)), ((), ()))
            acc = lax.dot_general(
                xbuf[:, a:b, :da].reshape(count, da), wgu[i, :, :da], contract,
                preferred_element_type=F32,
            ) + lax.dot_general(
                xbuf[:, a:b, ext:].reshape(count, 2 * WB), wgu[i, :, da:], contract,
                preferred_element_type=F32,
            )
            g, u = acc[:, :LANES], acc[:, LANES:]
            shares = xbuf[:, a:b, da:ext].reshape(count, LANES)

            def hit(e, j):
                at = j + i * LANES - e * hidden
                return (at >= 0) & (at < hidden) & (e < local)

            scale = jnp.dot(
                shares, onehot(LANES, LANES, hit), preferred_element_type=F32
            )
            h = g / (1.0 + jnp.exp(-g)) * u * scale
            hbuf[:count, pl.ds(pl.multiple_of(i * LANES, LANES), LANES)] = h.astype(BF16)
            return _

        lax.fori_loop(first, first + count_tiles, hidden_tile, 0)

    def sent(c):
        for q in range(12):
            ag[c][q].wait_send()

    def down(c, q):
        a, b = chunks[c]
        span = b - a
        count = 8 * span
        tile = 512

        def down_tile(n, _):
            cols = pl.ds(pl.multiple_of(q * half + n * tile, tile), tile)
            out = jnp.dot(hbuf[:count, :], wd[:, cols], preferred_element_type=F32)
            xbuf[:, a:b, cols] = out.astype(BF16).reshape(8, span, tile)
            return _

        lax.fori_loop(0, half // tile, down_tile, 0)
        rows, cols = pl.ds(a, span), (low, high)[q]
        rs[c][q] = remote(
            xbuf.at[pl.ds(4, 4), rows, cols], pr.at[c % 2, :, pl.ds(0, span), cols],
            rss.at[c, q], rsv.at[c, q], partner,
        )
        rs[c][q].start()

    def add(dst, dst_at, srcs, a, b, low, high):
        tile = 512

        def step(n, _):
            cols = pl.ds(pl.multiple_of(low + n * tile, tile), tile)
            total = dst[dst_at, a:b, cols].astype(F32)
            for src in srcs:
                total = total + src(n * tile, tile).astype(F32)
            dst[dst_at, a:b, cols] = total.astype(BF16)
            return _

        lax.fori_loop(0, (high - low) // tile, step, 0)

    def cut(ref, lead, a, b, base):
        def get(at, size):
            cols = pl.ds(pl.multiple_of(base + at, size), size)
            return ref[a:b, cols] if lead is None else ref[lead, a:b, cols]

        return get

    def partner_sum(c, q):
        a, b = chunks[c]
        rows, cols = pl.ds(a, b - a), (low, high)[q]
        at, to = q * half, (q + 1) * half
        rs[c][q].wait_recv()
        far_to, landing = (right, ra) if q == 0 else (left, rb)
        near, near_to, near_at = (3, left, fr) if q == 0 else (1, right, fl)
        add(xbuf, 2, [cut(pr.at[c % 2, 2], None, 0, b - a, at)], a, b, at, to)
        rs[c][2 + q] = remote(
            xbuf.at[2, rows, cols], landing.at[rows], rss.at[c, 2 + q], rsv.at[c, 2 + q], far_to
        )
        rs[c][2 + q].start()
        add(xbuf, near, [cut(pr.at[c % 2, near], None, 0, b - a, at)], a, b, at, to)
        rs[c][4 + q] = remote(
            xbuf.at[near, rows, cols], near_at.at[rows, cols],
            rss.at[c, 4 + q], rsv.at[c, 4 + q], near_to,
        )
        rs[c][4 + q].start()
        add(xbuf, 4 - near, [cut(pr.at[c % 2, 4 - near], None, 0, b - a, at)], a, b, at, to)
        add(xbuf, 0, [cut(pr.at[c % 2, 0], None, 0, b - a, at)], a, b, at, to)

    def ring_sum(c):
        a, b = chunks[c]
        rows = pl.ds(a, b - a)
        for q, s, landed, to, at in ((0, 1, ra, right, fl), (1, 3, rb, left, fr)):
            cols = (low, high)[q]
            rs[c][2 + q].wait_recv()
            add(xbuf, s, [cut(landed, None, a, b, 0)], a, b, q * half, (q + 1) * half)
            rs[c][6 + q] = remote(
                xbuf.at[s, rows, cols], at.at[rows, cols], rss.at[c, 6 + q], rsv.at[c, 6 + q], to
            )
            rs[c][6 + q].start()

    def finish(c):
        a, b = chunks[c]
        for q in (4, 5, 6, 7):
            rs[c][q].wait_recv()
        add(xbuf, 0, [cut(fl, None, a, b, 0), cut(fr, None, a, b, 0)], a, b, 0, width)
        p0 = state["returned"]
        p1 = b // CAP
        state["returned"] = p1
        w0 = p0 * CAP // 16 * 16

        def hit(i, j):
            match = None
            for p in range(p0, p1):
                s = i - (p - p0) * SLOTS
                m = (s >= 0) & (s < CAP) & (j + w0 == s + p * CAP)
                match = m if match is None else match | m
            return match

        spread = onehot((p1 - p0) * SLOTS, b - w0, hit)
        tile = 1280

        def step(n, _):
            cols = pl.ds(pl.multiple_of(n * tile, tile), tile)
            out = jnp.dot(spread, xbuf[0, w0:b, cols], preferred_element_type=F32)
            exr[p0 * SLOTS : p1 * SLOTS, cols] = out.astype(BF16)
            return _

        lax.fori_loop(0, width // tile, step, 0)
        for p in range(p0, p1):
            block = pl.ds(p * SLOTS, SLOTS)
            if p == 0:
                back[:SLOTS, :] = exr[:SLOTS, :width]
            else:
                ret[p] = remote(
                    exr.at[block, pl.ds(0, width)], back.at[block], rts.at[p], rtv.at[p], back_there(p)
                )
                ret[p].start()

    last = len(chunks) - 1
    exchange_rows(0)
    row[0].wait_recv()
    row[2].start()
    row[3].start()
    exchange_rows(1)
    selectors(0)
    row[1].wait_recv()
    row[5].start()
    row[3].wait_recv()
    row[6].start()
    own(0)
    row[2].wait_recv()
    selectors(3)
    row[4].wait_recv()
    selectors(1)
    row[5].wait_recv()
    row[6].wait_recv()
    selectors(2)
    build(0)
    exchange_rows(2)
    build(1)
    relay(0)
    own(1)
    for c in range(3, len(chunks)):
        exchange_rows(c)
    forward(0)
    take(0)
    for w in weights:
        w.wait()
    for c in range(len(chunks)):
        far(c)
        gated(c, 0, 2)
        if c + 1 <= last:
            relay(c + 1)
        if c + 2 <= last:
            own(c + 2)
            build(c + 2)
        gated(c, 2, tiles - 2)
        if c + 1 <= last:
            forward(c + 1)
        if c >= 2:
            finish(c - 2)
        if c >= 1:
            ring_sum(c - 1)
        sent(c)
        down(c, 0)
        down(c, 1)
        partner_sum(c, 0)
        partner_sum(c, 1)
        if c + 1 <= last:
            take(c + 1)
    finish(last - 1)
    ring_sum(last)
    finish(last)
    for q in row:
        q.wait_send()
    for p in range(max(starts[-3], 1), nodes):
        bsend[p].wait_send()
    for p in range(1, nodes):
        exchange[p].wait_send()
    for c in range(len(chunks)):
        for q in range(8):
            rs[c][q].wait_send()
    for p in range(1, nodes):
        ret[p].wait_send()
        ret[p].wait_recv()

    def unpack(n, _):
        cols = pl.ds(pl.multiple_of(n * 1280, 1280), 1280)
        out_ref[:, cols] = jnp.dot(
            spread_rows, back[:, cols], preferred_element_type=F32
        ).astype(BF16)
        return _

    lax.fori_loop(0, width // 1280, unpack, 0)


def shards(tokens, node_ids, expert_pick, gate_share, gate_proj, up_proj, down_proj):
    tok_count, width = tokens.shape
    local, hidden, _ = gate_proj.shape
    nodes = len(HOPS)
    rows = nodes * CAP
    chunks = len(CUTS) - 1
    most = max(b - a for a, b in zip(CUTS[:-1], CUTS[1:]))
    starts = [0] + [(b - 1) // CAP + 1 for b in CUTS[1:]]
    groups = max(b - a for a, b in zip(starts[:-1], starts[1:]))
    tiles = -(-local * hidden // LANES)
    dma = pltpu.SemaphoreType.DMA
    vmem, anywhere = pl.BlockSpec(memory_space=pltpu.VMEM), pl.BlockSpec(memory_space=pl.ANY)
    return pl.pallas_call(
        kernel,
        out_shape=jax.ShapeDtypeStruct((tok_count, width), BF16),
        in_specs=[vmem] * 3 + [anywhere] * 4,
        out_specs=vmem,
        scratch_shapes=[
            pltpu.VMEM((tok_count, width), BF16),
            pltpu.VMEM((nodes * SLOTS, width - 2 * WB + LANES), BF16),
            pltpu.VMEM((4, 2 * tok_count, WB + LANES), BF16),
            pltpu.VMEM((tok_count, WB + LANES), BF16),
            pltpu.VMEM((8, nodes * SLOTS, tok_count), BF16),
            pltpu.VMEM((2, groups, 8, SLOTS, WB), BF16),
            pltpu.VMEM((nodes, 8, SLOTS, WB), BF16),
            pltpu.VMEM((nodes * SLOTS, width), BF16),
            pltpu.VMEM((tiles, 2 * LANES, width), BF16),
            pltpu.VMEM((tiles * LANES, width), BF16),
            pltpu.VMEM((8, rows, width + LANES), BF16),
            pltpu.VMEM((nodes * SLOTS, width), BF16),
            pltpu.VMEM((2, 4, most, width), BF16),
            pltpu.VMEM((rows, width // 2), BF16),
            pltpu.VMEM((rows, width // 2), BF16),
            pltpu.VMEM((rows, width), BF16),
            pltpu.VMEM((rows, width), BF16),
            pltpu.VMEM((8 * most, tiles * LANES), BF16),
            dma((3,)),
            dma((7,)),
            dma((7,)),
            dma((nodes,)),
            dma((nodes,)),
            dma((local * (6 * (hidden // BLOCK) + 1),)),
            dma((nodes,)),
            dma((nodes,)),
            dma((chunks, 12)),
            dma((chunks, 12)),
            dma((chunks, 8)),
            dma((chunks, 8)),
            dma((nodes,)),
            dma((nodes,)),
        ],
        compiler_params=pltpu.CompilerParams(
            collective_id=0, has_side_effects=True, vmem_limit_bytes=67_043_328
        ),
        name="routed_experts",
    )(node_ids, expert_pick, gate_share, tokens, gate_proj, up_proj, down_proj)


def solution(mesh):
    return jax.shard_map(
        shards,
        mesh=mesh,
        in_specs=(
            P(("node", "dev"), None),
            P(("node", "dev"), None),
            P(("node", "dev"), None),
            P(("node", "dev"), None),
            P("node", "dev", None),
            P("node", "dev", None),
            P("node", "dev", None),
        ),
        out_specs=P(("node", "dev"), None),
        check_vma=False,
    )
```

time: 210 us -> 177 us (0.84)
  Pallas kernels: 199 us -> 169 us
  local copies, waits for them, and re-layouts: 0.63 us -> 6.1 us
  matrix products: 5.41 us -> 0 us
  other arithmetic: 4.68 us -> 0 us
    pallas_call x1, Pallas kernels: 199 us -> 169 us  [shards(): pl.pallas_call(kernel, out_shape=jax.ShapeDtypeStruct((tok_count, width),...]
    unnamed x2 -> x4, local copies, waits for them, and re-layouts: 0.33 us -> 6.1 us
    dot_general x4 -> x0, matrix products: 5.41 us -> none  [the longest x1 3.21 us: shards(): lax.dot_general(flat, back.reshape(nodes * SLOTS, width), (((0,), (0,)),...]
where the time goes in v1:
time: 177 us; the launch traced here: 175 us
  Pallas kernels  169 us (95%)
  local copies, waits for them, and re-layouts  6.1 us (3%)
    pallas_call x1, Pallas kernels, shards(): pl.pallas_call(kernel, out_shape=jax.ShapeDtypeStruct((tok_count, width),...  169 us
    unnamed x4, local copies, waits for them, and re-layouts  6.1 us

profile of v1, /device:TPU:34, one launch (start us, length us, event | category | flops | bytes accessed | tf_op | source)
XLA Modules:
  0.0 175.4 jit_solution(852113521087777443)
XLA Ops:
  0.0 1.4 copy.10.share_ref
  1.4 1.4 copy.8.ids_ref
  2.8 1.4 copy.9.pick_ref
  4.1 169.3 %routed_experts.1 = bf16[64,5120]{1,0:T(8,128)(2,1)} custom-call(s32[64,3]{1,0:T(8,128)} %copy.8.ids_ref, s32[64,6]{1,0:T(8,128)} %copy.9.pick_ref, bf16[64,6]{1,0:T(8,128)(2,1)} %copy.10.share_ref, bf16[64,5120]{1,0:T(8,128)(2,1)} %tok_ref.1, bf16[3,192,5120]{2,1,0:T(8,128)(2,1)} %gate_ref.1, bf16[3,192,5120]{2,1,0:T(8,128)(2,1)} %up_ref.1, ...), custom_call_target="tpu_custom_call" | custom-call | tf_op jit(solution)/shard_map/routed_experts/pallas_call | solution.py:563
  173.5 2.0 %copy.12 = bf16[64,5120]{1,0:T(8,128)(2,1)} copy(bf16[64,5120]{1,0:T(8,128)(2,1)} %routed_experts.1) | data formatting | bytes 1310720

commit v2 on v1

--- a/solution.py
+++ b/solution.py
@@ -15,7 +15,7 @@
 F32 = jnp.float32
 BF16 = jnp.bfloat16
 MESH = pl.DeviceIdType.MESH
-CUTS = (0, 48, 112, 176, 208)
+CUTS = (0, 48, 112, 160, 208)
 HOPS = (
     (0, 0), (0, 1), (1, 0), (0, 3), (1, 1), (3, 3), (0, 2), (2, 0),
     (1, 2), (2, 3), (2, 1), (3, 2), (2, 2), (3, 1), (1, 3), (3, 0),

time: 177 us -> 174 us (0.983)
  Pallas kernels: 169 us -> 165 us
    pallas_call x1, Pallas kernels: 169 us -> 165 us  [shards(): pl.pallas_call(kernel, out_shape=jax.ShapeDtypeStruct((tok_count, width),...]
where the time goes in v2:
time: 174 us; the launch traced here: 171 us
  Pallas kernels  165 us (95%)
  local copies, waits for them, and re-layouts  6.1 us (4%)
    pallas_call x1, Pallas kernels, shards(): pl.pallas_call(kernel, out_shape=jax.ShapeDtypeStruct((tok_count, width),...  165 us
    unnamed x4, local copies, waits for them, and re-layouts  6.1 us

profile of v2, /device:TPU:34, one launch (start us, length us, event | category | flops | bytes accessed | tf_op | source)
XLA Modules:
  0.0 171.5 jit_solution(17952975268191686034)
XLA Ops:
  0.0 1.4 copy.10.share_ref
  1.4 1.4 copy.8.ids_ref
  2.8 1.4 copy.9.pick_ref
  4.1 165.4 %routed_experts.1 = bf16[64,5120]{1,0:T(8,128)(2,1)} custom-call(s32[64,3]{1,0:T(8,128)} %copy.8.ids_ref, s32[64,6]{1,0:T(8,128)} %copy.9.pick_ref, bf16[64,6]{1,0:T(8,128)(2,1)} %copy.10.share_ref, bf16[64,5120]{1,0:T(8,128)(2,1)} %tok_ref.1, bf16[3,192,5120]{2,1,0:T(8,128)(2,1)} %gate_ref.1, bf16[3,192,5120]{2,1,0:T(8,128)(2,1)} %up_ref.1, ...), custom_call_target="tpu_custom_call" | custom-call | tf_op jit(solution)/shard_map/routed_experts/pallas_call | solution.py:563
  169.5 2.0 %copy.12 = bf16[64,5120]{1,0:T(8,128)(2,1)} copy(bf16[64,5120]{1,0:T(8,128)(2,1)} %routed_experts.1) | data formatting | bytes 1310720
